TPU v7x, 256 devices: a 8x8x2 block of a 8x8x16 slice. The times are simulated.
256 devices in a mesh: grp: 2 (over z), row: 16 (over x, core), col: 8 (over y).
Axes of the slice: x: 8, y: 8, z: 2, core: 2. Of those that a mesh axis runs over, the one named last changes fastest.
The devices are a block of a 8x8x16 slice.
Arguments:
- perturbation: bfloat16 [4, 12000, 12000], P('grp', 'row', 'col'), parts along dimension 0, may hold values from -96 to 96
- occ_coeffs: bfloat16 [12000, 2000], P('row', 'col'), may hold values from -0.0546875 to 0.0546875
- vir_coeffs: bfloat16 [12000, 512], P('col', 'row'), may hold values from -0.0546875 to 0.0546875
- occ_energies: float32 [2000], replicated, may hold values from -1 to -0.1
- vir_energies: float32 [512], replicated, may hold values from 0.1 to 1.5
Outputs:
- density_response: bfloat16 [4, 12000, 12000], P('grp', 'row', 'col'), parts along dimension 0
There are 2 independent parts, one for each index of `grp`. A program takes and returns all parts, laid end to end along the dimension named above; an argument that names none is the same for every part. Nothing has to cross between parts.
All inputs are finite; a program needn't handle non-finite values.
Results may differ from a plain program's by a relative error of at most 0.0098.
Values may be sent and summed in bfloat16 or wider, within the bound.
A program may use at most 64 MiB of HBM per device.

v0:
```python
import jax
import jax.numpy as jnp
from jax import lax
from jax.sharding import Mesh
from jax.sharding import PartitionSpec as P

ROW = ("row_0", "row_1")


def joined_along(pieces, dim):
    pieces = jnp.moveaxis(pieces, 0, dim)
    dims = pieces.shape
    return pieces.reshape(*dims[:dim], dims[dim] * dims[dim + 1], *dims[dim + 2 :])


def sent_to_all(shard, axis):
    copies = jnp.broadcast_to(shard, (lax.axis_size(axis), *shard.shape))
    return lax.all_to_all(copies, axis, split_axis=0, concat_axis=0, tiled=True)


def collect(shard, axis, dim):
    return joined_along(sent_to_all(shard, axis), dim)


def cut_along(shard, dim, count):
    before, after = (shard.shape[:dim], shard.shape[dim + 1 :])
    return jnp.moveaxis(shard.reshape(*before, count, -1, *after), dim, 0)


def summed_on_arrival(shard, axis, dim):
    count = lax.axis_size(axis)
    pieces = lax.all_to_all(cut_along(shard, dim, count), axis, 0, 0, tiled=True)
    return jnp.sum(pieces.astype(jnp.float32), axis=0)


def padded_to(lines, count):
    spare = -len(lines) % count
    return jnp.pad(lines, [(0, spare)] + [(0, 0)] * (lines.ndim - 1))


def reduced_to_own(pieces, axes, order):
    inside = pieces.shape[1:]
    pieces = pieces.reshape(*(lax.axis_size(a) for a in axes), *inside)
    pieces = jnp.moveaxis(pieces, order, range(len(axes))).reshape(-1, *inside)
    for k in order:
        pieces = lax.psum_scatter(pieces, axes[k], scatter_dimension=0, tiled=True)
    return pieces[0]


def stacked_from(shard, axes, order):
    pieces = shard[None]
    for k in order:
        pieces = lax.all_gather(pieces, axes[k], axis=0, tiled=True)
    carried = [lax.axis_size(axes[k]) for k in reversed(order)]
    pieces = pieces.reshape(*carried, *shard.shape)
    turned = sorted(range(len(order)), key=lambda place: order[len(order) - 1 - place])
    return pieces.transpose(*turned, *range(len(order), pieces.ndim)).reshape(-1, *shard.shape)


def sum_by_parts(shard, axes, order):
    count, lines = (lax.axis_size(axes), shard.reshape(-1, *shard.shape[1:][-1:]))
    pieces = padded_to(lines, count).reshape(count, -1, *lines.shape[1:])
    own = reduced_to_own(pieces, axes, order)
    whole = stacked_from(own, axes, order[::-1]).reshape(-1, *lines.shape[1:])
    return whole[: len(lines)].reshape(shard.shape)


def per_device(perturbation, occ_coeffs, vir_coeffs, occ_energies, vir_energies):
    occ_rows = lax.all_gather(occ_coeffs, "col", axis=1, tiled=True)
    vir_rows = collect(vir_coeffs, ROW, 1)
    share = vir_rows.shape[1] // lax.axis_size("col")
    image = summed_on_arrival(
        jnp.einsum(
            "pij,jv->vpi", perturbation, vir_rows, preferred_element_type=jnp.float32
        ).astype(jnp.bfloat16),
        "col",
        0,
    )
    partial_value = jnp.einsum(
        "io,vpi->pov", occ_rows.astype(jnp.float32), image, precision=lax.Precision.HIGHEST
    )
    coupling = sum_by_parts(partial_value, ROW, (0, 1))
    offset = lax.axis_index("col") * share
    energies = lax.dynamic_slice_in_dim(vir_energies, offset, share, 0)
    gaps = occ_energies[:, None] - energies[None, :]
    response = (coupling / gaps[None, :, :]).astype(jnp.bfloat16)
    mixed = jnp.einsum(
        "io,pov->piv", occ_rows, response, preferred_element_type=jnp.float32
    ).astype(jnp.bfloat16)
    total = jnp.einsum(
        "piv,jv->pij", collect(mixed, "col", 2), vir_rows, preferred_element_type=jnp.float32
    )
    return total.astype(jnp.bfloat16)


def solution(mesh):
    torus = Mesh(
        mesh.devices.reshape(mesh.shape["grp"], 8, 2, mesh.shape["col"]),
        ("grp", "row_0", "row_1", "col"),
    )
    in_specs = (P("grp", ROW, "col"), P(ROW, "col"), P("col", ROW), P(), P())
    out_specs = P("grp", ROW, "col")
    return jax.shard_map(
        per_device, mesh=torus, in_specs=in_specs, out_specs=out_specs, check_vma=False
    )
```

profile of v0, /device:TPU:516, one launch (start us, length us, event | category | flops | bytes accessed | tf_op | source)
XLA Modules:
  0.0 288.0 jit_solution(6391762949328565553)
XLA Ops:
  6.5 2.2 broadcast_in_dim.4
  8.7 22.8 %all-to-all-start = ((bf16[16,1500,32]{1,2,0:T(8,128)(2,1)}), bf16[16,1500,32]{1,2,0:T(8,128)(2,1)S(1)}, u32[]{:S(2)}, u32[]{:S(2)}) async-start(bf16[16,1500,32]{1,2,0:T(8,128)(2,1)} %broadcast_in_dim.4), calls=%async_computation | async-start | bytes 3145728 | tf_op jit(solution)/shard_map/all_to_all | solution.py:18
  31.6 0.7 all-gather.3.cloned.1.call-update
  32.3 35.1 %all-to-all-done = bf16[16,1500,32]{1,2,0:T(8,128)(2,1)S(1)} async-done(((bf16[16,1500,32]{1,2,0:T(8,128)(2,1)}), bf16[16,1500,32]{1,2,0:T(8,128)(2,1)S(1)}, u32[]{:S(2)}, u32[]{:S(2)}) %all-to-all-start) | async-done | bytes 1536032 | tf_op jit(solution)/shard_map/all_to_all | solution.py:18
  67.4 1.1 copy-done
  68.6 4.9 %fusion.9 = bf16[512,2,750]{0,2,1:T(8,128)(2,1)S(1)} fusion(bf16[1500,512,1]{0,1,2:T(8,128)(2,1)S(1)} %bitcast.40, bf16[2,750,1500]{2,0,1:T(2,128)(2,1)} %param.5), kind=kOutput, calls=%fused_computation.9 | convolution fusion | flops 2304768000 | bytes 7572000 | tf_op jit(solution)/shard_map/pij,jv->vpi/dot_general | solution.py:73
  73.5 0.7 copy.24
  74.2 1.3 copy.25
  75.5 4.5 %all-to-all-start.1 = ((bf16[8,64,2,750]{3,1,2,0:T(8,128)(2,1)}), bf16[8,64,2,750]{3,1,2,0:T(8,128)(2,1)}, u32[]{:S(2)}, u32[]{:S(2)}) async-start(bf16[8,64,2,750]{3,1,2,0:T(8,128)(2,1)} %copy.25), calls=%async_computation.1 | async-start | bytes 3145728 | tf_op jit(solution)/shard_map/all_to_all | solution.py:32
  80.0 2.3 all-gather.3.cloned.1.call-done
  82.3 4.6 %copy.26 = bf16[8,250,750]{1,0,2:T(8,128)(2,1)} copy(bf16[8,250,750]{1,2,0:T(8,128)(2,1)} %all-gather.3.cloned.1.call-done) | data formatting | bytes 6000000 | tf_op jit(solution)/shard_map/all_gather | solution.py:69
  86.9 5.5 %reshape.42 = bf16[2000,750]{0,1:T(8,128)(2,1)S(1)} reshape(bf16[8,250,750]{1,0,2:T(8,128)(2,1)} %copy.26) | data formatting | bytes 6000000
  92.4 28.9 %all-to-all-done.1 = bf16[8,64,2,750]{3,1,2,0:T(8,128)(2,1)} async-done(((bf16[8,64,2,750]{3,1,2,0:T(8,128)(2,1)}), bf16[8,64,2,750]{3,1,2,0:T(8,128)(2,1)}, u32[]{:S(2)}, u32[]{:S(2)}) %all-to-all-start.1) | async-done | bytes 1536032 | tf_op jit(solution)/shard_map/all_to_all | solution.py:32
  121.3 1.7 convert_reduce_fusion
  123.0 1.5 fusion.6
  124.4 1.8 copy.28
  126.2 3.5 %reshape_reshape_reshape.3 = f32[16,250,64]{1,0,2:T(8,128)} reshape(f32[2,2000,64]{1,0,2:T(2,128)} %copy.28) | data formatting | bytes 2048000 | tf_op jit(solution)/shard_map/reshape;reshape;reshape | solution.py:44
  129.7 2.8 copy.29
  132.6 0.8 dynamic_slice.3
  133.4 36.3 %reduce-scatter.3.cloned.1.call-done = f32[2,250,64]{1,2,0:T(8,128)} async-done(((f32[16,250,64]{1,2,0:T(8,128)}), f32[2,250,64]{1,2,0:T(8,128)}) %reduce-scatter.3.cloned.1.call-update) | async-done | bytes 128016 | tf_op jit(solution)/shard_map/reduce_scatter | solution.py:46
  169.7 0.9 broadcast_subtract_fusion
  170.7 16.2 %reduce-scatter.5.cloned.1.call-done = f32[1,250,64]{1,2,0:T(8,128)} async-done(((f32[2,250,64]{1,2,0:T(8,128)}), f32[1,250,64]{1,2,0:T(8,128)}) %reduce-scatter.5.cloned.1.call-update) | async-done | bytes 64016 | tf_op jit(solution)/shard_map/reduce_scatter | solution.py:46
  186.9 2.1 all_gather.10
  189.0 28.1 %all_gather.11 = f32[16,250,64]{1,2,0:T(8,128)S(1)} all-gather(f32[2,250,64]{1,2,0:T(8,128)S(1)} %all_gather.10), channel_id=1, replica_groups=mesh['grp'=2,'row_0'=8,'row_1'=2,'col'=8] {'row_0'}, dimensions={0}, use_global_device_ids=true | all-gather | bytes 1152000 | tf_op jit(solution)/shard_map/all_gather | solution.py:53
  217.1 1.6 copy.30
  218.7 3.7 %reshape_reshape_reshape_reshape.3 = f32[2,2000,64]{1,0,2:T(2,128)} reshape(f32[16,250,64]{1,0,2:T(8,128)} %copy.30) | data formatting | bytes 2048000 | tf_op jit(solution)/shard_map/reshape;reshape;reshape;reshape | solution.py:65
  222.4 1.9 divide_convert_fusion
  224.3 1.1 fusion.15
  225.4 0.1 broadcast_in_dim.10
  225.5 41.8 %all_to_all.15 = bf16[8,2,750,64]{2,3,1,0:T(8,128)(2,1)S(1)} all-to-all(bf16[8,2,750,64]{2,3,1,0:T(8,128)(2,1)S(1)} %broadcast_in_dim.10), channel_id=1, replica_groups=mesh['grp'=2,'row_0'=8,'row_1'=2,'col'=8] {'col'}, dimensions={0} | all-to-all | bytes 3072000 | tf_op jit(solution)/shard_map/all_to_all | solution.py:18
  267.5 4.7 %convolution_convert_fusion = bf16[2,750,1500]{2,1,0:T(8,128)(2,1)} fusion(bf16[2,750,512]{1,2,0:T(8,128)(2,1)S(1)} %bitcast.42, bf16[1500,512,1]{0,1,2:T(8,128)(2,1)S(1)} %bitcast.41), kind=kOutput, calls=%fused_computation.2 | convolution fusion | flops 2306249984 | bytes 7572000 | tf_op jit(solution)/shard_map/piv,jv->pij/dot_general | solution.py:90
  272.2 9.2 %copy.36 = bf16[2,750,1500]{2,0,1:T(2,128)(2,1)} copy(bf16[2,750,1500]{2,1,0:T(8,128)(2,1)} %convolution_convert_fusion) | data formatting | bytes 9000000 | tf_op jit(solution)/shard_map/convert_element_type | solution.py:93
  (11 shorter events, 0.4 us)
Async XLA Ops:
  8.7 58.7 %all-to-all-start = ((bf16[16,1500,32]{1,2,0:T(8,128)(2,1)}), bf16[16,1500,32]{1,2,0:T(8,128)(2,1)S(1)}, u32[]{:S(2)}, u32[]{:S(2)}) async-start(bf16[16,1500,32]{1,2,0:T(8,128)(2,1)} %broadcast_in_dim.4), calls=%async_computation | async-start | bytes 3145728 | tf_op jit(solution)/shard_map/all_to_all | solution.py:18
  31.5 50.8 %all-gather.3.cloned.1.call-start = ((), (), s32[]{:S(2)}) async-start(), calls=%async_computation.7 | async-start | bytes 3465216 | tf_op jit(solution)/shard_map/all_gather | solution.py:69
  67.4 1.2 copy-start
  75.5 45.8 %all-to-all-start.1 = ((bf16[8,64,2,750]{3,1,2,0:T(8,128)(2,1)}), bf16[8,64,2,750]{3,1,2,0:T(8,128)(2,1)}, u32[]{:S(2)}, u32[]{:S(2)}) async-start(bf16[8,64,2,750]{3,1,2,0:T(8,128)(2,1)} %copy.25), calls=%async_computation.1 | async-start | bytes 3145728 | tf_op jit(solution)/shard_map/all_to_all | solution.py:32
  80.0 89.7 %reduce-scatter.3.cloned.1.call-start = ((), (), s32[]{:S(2)}) async-start(), calls=%async_computation.5 | async-start | bytes 1179648 | tf_op jit(solution)/shard_map/reduce_scatter | solution.py:46
  126.2 43.5 %copy-start.2 = (f32[2000]{0:T(1024)S(1)}, f32[2000]{0:T(1024)}, u32[]{:S(2)}) copy-start(f32[2000]{0:T(1024)} %param.8) | copy-start | bytes 24004
  132.6 54.3 %reduce-scatter.5.cloned.1.call-start = ((), (), s32[]{:S(2)}) async-start(), calls=%async_computation.6 | async-start | bytes 196608 | tf_op jit(solution)/shard_map/reduce_scatter | solution.py:46
  225.5 42.0 %copy-start.1 = (bf16[16,1500,32]{1,2,0:T(8,128)(2,1)S(1)}, bf16[16,1500,32]{1,2,0:T(8,128)(2,1)}, u32[]{:S(2)}) copy-start(bf16[16,1500,32]{1,2,0:T(8,128)(2,1)} %copy-done) | copy-start | bytes 4608004
Sparse Core Ops, SparseCore 0:
  34.2 48.1 all-gather.2
  132.7 36.9 reduce-scatter.2
  172.1 14.6 reduce-scatter.4
where the time goes:
time: 289 us; the launch traced here: 288 us
  waiting for transfers between devices  120 us (42%)
  blocking collectives  72.1 us (25%)
  local copies, waits for them, and re-layouts  38.9 us (13%)
  starting transfers between devices  27.4 us (9%)
  between operations  13.2 us (5%)
  matrix products  12.2 us (4%)
  other arithmetic  4.5 us (2%)
    reduce_scatter x2, waiting for transfers between devices, reduced_to_own(): pieces = lax.psum_scatter(pieces, axes[k], scatter_dimension=0, tiled=True)  52.5 us
    all_to_all x1, blocking collectives, sent_to_all(): return lax.all_to_all(copies, axis, split_axis=0, concat_axis=0, tiled=True)  41.8 us
    all_to_all x1, waiting for transfers between devices, sent_to_all(): return lax.all_to_all(copies, axis, split_axis=0, concat_axis=0, tiled=True)  35.1 us
    all_gather x2, blocking collectives, stacked_from(): pieces = lax.all_gather(pieces, axes[k], axis=0, tiled=True)  30.3 us
    all_to_all x1, waiting for transfers between devices, summed_on_arrival(): lax.all_to_all(cut_along(shard, dim, count), axis, 0, 0, tiled=True)  28.9 us
    all_to_all x1, starting transfers between devices, sent_to_all(): return lax.all_to_all(copies, axis, split_axis=0, concat_axis=0, tiled=True)  22.8 us
    convert_element_type x1, local copies, waits for them, and re-layouts, per_device(): return total.astype(jnp.bfloat16)  9.19 us
    unnamed x7, local copies, waits for them, and re-layouts  6.63 us
  transfers between devices with their start and end apart: 5, of which 5 were waited for; matrix products, arithmetic and copies ran while one was open for 6% of the time, Pallas kernels for 0%

commit v1 on v0

v1 whole, which is shorter than its diff:
```python
import functools

import jax
import jax.numpy as jnp
from jax import lax
from jax.experimental import pallas as pl
from jax.experimental.pallas import tpu as pltpu
from jax.sharding import PartitionSpec as P

MESH = pl.DeviceIdType.MESH
BF16, F32 = jnp.bfloat16, jnp.float32
LANES = 128
NT = (((1,), (1,)), ((), ()))


def round_up(n, m):
    return -(-n // m) * m


def exchange_kernel(dims, *refs):
    nrow, ncol, rows, cols, occ, vir = dims
    (h_hbm, vt_ref, c_ref, eo_ref, ev_ref, mix_ref, vtall_ref) = refs[:7]
    (hbuf, xs, xo, cbuf, rs0, rsb, ct, cx, red, xr, rb, eo_pad) = refs[7:19]
    (h_sem, v_s, v_r, vd_s, vd_r, c_s, c_r, r_s, r_r) = refs[19:28]
    (d_s, d_r, a_s, a_r, g_s, g_r, e_s, e_r, m_s, m_r) = refs[28:]

    nx = nrow // 2
    half = ncol // 2
    hx = nx // 2
    mine = vt_ref.shape[0]
    padded = cbuf.shape[1]
    cut = rs0.shape[2]
    chunks = ((0, cut), (cut, padded - cut))

    r = lax.axis_index("row")
    y = lax.axis_index("col")
    x = lax.div(r, 2)
    k = lax.rem(r, 2)

    def at_y(m):
        return lax.rem(y + m + ncol, ncol)

    def at_x(m):
        return lax.rem(x + m + nx, nx)

    up, down = {"col": at_y(1)}, {"col": at_y(-1)}
    y_next = (up, down)
    x_next = ({"row": 2 * at_x(1) + k}, {"row": 2 * at_x(-1) + k})
    partner = {"row": 2 * x + 1 - k}

    def remote(src, dst, ss, rr, dev):
        return pltpu.make_async_remote_copy(
            src_ref=src, dst_ref=dst, send_sem=ss, recv_sem=rr, device_id=dev, device_id_type=MESH
        )

    h_copy = pltpu.make_async_copy(h_hbm, hbuf, h_sem)
    h_copy.start()

    barrier = pltpu.get_barrier_semaphore()
    for dev in y_next:
        pl.semaphore_signal(barrier, inc=1, device_id=dev, device_id_type=MESH)
    for j in range(1, nrow):
        pl.semaphore_signal(
            barrier, inc=1, device_id={"row": lax.rem(r + j, nrow)}, device_id_type=MESH
        )

    nocc = c_ref.shape[1]
    wide = cbuf.shape[2]
    cbuf[y, :, pl.ds(wide - LANES, LANES)] = jnp.zeros((padded, LANES), BF16)
    cbuf[y, pl.ds(padded - 16, 16), :] = jnp.zeros((16, wide), BF16)
    cbuf[y, pl.ds(0, rows), pl.ds(0, nocc)] = c_ref[...]
    vtall_ref[pl.ds(pl.multiple_of(r * mine, mine), mine), :] = vt_ref[...]

    eo_pad[...] = jnp.full(eo_pad.shape, -1.0, F32)
    eo_pad[:, pl.ds(0, occ)] = eo_ref[...]
    first = x * nocc + k * LANES
    near = pl.multiple_of(lax.div(first, LANES) * LANES, LANES)
    window = eo_pad[:, pl.ds(near, 2 * LANES)]
    window = pltpu.roll(
        jnp.broadcast_to(window, (8, 2 * LANES)), 2 * LANES - lax.rem(first, LANES), 1
    )
    eo = jnp.broadcast_to(window[0:1, 0:LANES], (LANES, LANES))
    ev = ev_ref[:, pl.ds(pl.multiple_of(lax.div(y, 2) * LANES, LANES), LANES)]
    ev = jnp.broadcast_to(ev, (LANES, LANES)).T
    gap = eo - ev

    pl.semaphore_wait(barrier, nrow + 1)

    def ring(buf, ss, rr):
        def copy(d, s, c, back):
            m = (s - 1) + back
            origin = at_y(-m) if d == 0 else at_y(m)
            n = 2 * (s - 1) + (c if s < half else 0)
            part = buf.at[origin, pl.ds(chunks[c][0], chunks[c][1])]
            return remote(part, part, ss.at[d, n], rr.at[d, n], y_next[d])

        def send(d, s, c):
            copy(d, s, c, 0).start()

        def arrived(d, s, c):
            copy(d, s, c, 1).wait_recv()

        def drain():
            for d in range(2):
                for s in range(1, half + 1):
                    for c in range(2) if s < half else (d,):
                        copy(d, s, c, 0).wait_send()

        return send, arrived, drain

    c_send, c_arrived, c_drain = ring(cbuf, c_s, c_r)
    for c in range(2):
        for d in range(2):
            c_send(d, 1, c)

    hm = mine // 2

    def v_copy(d, s, c, back):
        m = (s - 1) + back
        origin = at_x(-m) if d == 0 else at_x(m)
        n = 2 * (s - 1) + (c if s < hx else 0)
        start = pl.multiple_of((2 * origin + k) * mine + c * hm, hm)
        part = vtall_ref.at[pl.ds(start, hm)]
        return remote(part, part, v_s.at[d, n], v_r.at[d, n], x_next[d])

    def v_over(n, m, other):
        kk = 1 - k if other else k
        start = pl.multiple_of((2 * at_x(m) + kk) * mine, mine)
        part = vtall_ref.at[pl.ds(start, mine)]
        return remote(part, part, vd_s.at[n], vd_r.at[n], partner)

    for c in range(2):
        for d in range(2):
            v_copy(d, 1, c, 0).start()
    v_over(0, 0, False).start()
    over = [(0, 0)]

    def c_forward(s, c):
        for d in range(2):
            c_arrived(d, s, c)
            if s + 1 < half or c == d:
                c_send(d, s + 1, c)

    for s in range(1, hx):
        for c in range(2):
            for d in range(2):
                v_copy(d, s, c, 1).wait_recv()
                if s + 1 < hx or c == d:
                    v_copy(d, s + 1, c, 0).start()
        for d in range(2):
            n, m = len(over), (-s if d == 0 else s)
            v_over(n, m, False).start()
            over.append((n, m))
        if s == hx - 2:
            c_forward(1, 0)
    c_forward(1, 1)
    for d in range(2):
        v_copy(d, hx, d, 1).wait_recv()
    v_over(len(over), hx, False).start()
    over.append((len(over), hx))
    for n, m in over:
        v_over(n, m, True).wait_recv()
    h_copy.wait()

    tile = 128
    tiles = -(-rows // tile)
    for t in range(tiles):
        if t == tiles // 2:
            c_forward(2, 0)
        i0 = min(t * tile, rows - tile)
        lhs = hbuf[pl.ds(i0, tile), :, :].reshape(2 * tile, cols)
        part = lax.dot_general(lhs, vtall_ref[...], NT, preferred_element_type=F32)
        for n in range(vir // LANES):
            xs[n, pl.ds(2 * i0, 2 * tile), :] = part[:, n * LANES : (n + 1) * LANES]
    c_forward(2, 1)
    for n in range(vir // LANES):
        xs[n, pl.ds(2 * rows, 2 * (padded - rows)), :] = jnp.zeros((2 * (padded - rows), LANES), F32)
    for n in range(ncol):
        xo[n] = xs.at[n // 2][pl.ds(n % 2, padded, stride=2), :]

    base = ((0, half), (0, half - 1))

    def length(d, c):
        return half if d == c else half - 1

    def slot(d, c, s):
        return base[d][c] + s - 1

    def own(m, c):
        return xo[at_y(m), pl.ds(*chunks[c]), :]

    def r_copy(d, c, s):
        n = slot(d, c, s)
        size = pl.ds(0, chunks[c][1])
        src = rs0.at[d, c, size] if s == 1 else rsb.at[d, slot(d, c, s - 1), size]
        return remote(src, rsb.at[d, n, size], r_s.at[d, n], r_r.at[d, n], y_next[d])

    chains = ((0, 0), (1, 1), (0, 1), (1, 0))
    for d, c in chains:
        m = length(d, c)
        rs0[d, c, pl.ds(0, chunks[c][1]), :] = own(m if d == 0 else -m, c).astype(BF16)
        r_copy(d, c, 1).start()
    for s in range(1, half):
        for d, c in chains:
            if s < length(d, c):
                r_copy(d, c, s).wait_recv()
                m = length(d, c) - s
                at = (d, slot(d, c, s), pl.ds(0, chunks[c][1]))
                rsb[at] = (rsb[at].astype(F32) + own(m if d == 0 else -m, c)).astype(BF16)
                r_copy(d, c, s + 1).start()
        if s == half - 2:
            c_forward(half - 1, 0)
            c_forward(half - 1, 1)
    image = []
    for c in range(2):
        total = own(0, c)
        for d in range(2):
            r_copy(d, c, length(d, c)).wait_recv()
            at = (d, slot(d, c, length(d, c)), pl.ds(0, chunks[c][1]))
            total = total + rsb[at].astype(F32)
        image.append(total)
    image = jnp.concatenate(image, axis=0).T.astype(BF16)

    for d in range(2):
        c_arrived(d, half, d)

    for b in range(ncol):
        part = jnp.dot(image, cbuf[b], preferred_element_type=F32).astype(BF16)
        ct[0, b] = part[:, 0:LANES]
        ct[1, b] = part[:, LANES:]
    pair = remote(ct.at[1 - k], cx, d_s, d_r, partner)
    pair.start()
    pair.wait_recv()
    red[...] = (ct[k].astype(F32) + cx[...].astype(F32)).astype(BF16)

    def a_copy(j):
        to = at_x(j)
        return remote(red.at[to], xr.at[j - 1], a_s.at[j - 1], a_r.at[j - 1], {"row": 2 * to + k})

    def g_copy(j, back):
        part = rb.at[k, at_x(-j) if back else x]
        return remote(part, part, g_s.at[j - 1], g_r.at[j - 1], {"row": 2 * at_x(j) + k})

    far = sorted(range(1, nx), key=lambda j: -min(j, nx - j))
    for j in far:
        a_copy(j).start()
    total = red[x].astype(F32)
    for j in reversed(far):
        a_copy(j).wait_recv()
        total = total + xr[j - 1].astype(F32)
    rb[k, x] = (total / gap).astype(BF16)
    for j in far:
        g_copy(j, False).start()
    for j in reversed(far):
        g_copy(j, True).wait_recv()
    give = remote(rb.at[k], rb.at[k], e_s, e_r, partner)
    give.start()
    take = remote(rb.at[1 - k], rb.at[1 - k], e_s, e_r, partner)
    take.wait_recv()

    mixed = jnp.zeros((padded, LANES), F32)
    for b in range(ncol):
        resp = jnp.concatenate([rb[0, b], rb[1, b]], axis=1)
        mixed = mixed + lax.dot_general(cbuf[b], resp, NT, preferred_element_type=F32)
    mix_ref[y] = mixed.astype(BF16)
    m_send, m_arrived, m_drain = ring(mix_ref, m_s, m_r)
    for c in range(2):
        for d in range(2):
            m_send(d, 1, c)
    for s in range(1, half):
        for c in range(2):
            for d in range(2):
                m_arrived(d, s, c)
                if s + 1 < half or c == d:
                    m_send(d, s + 1, c)
    for d in range(2):
        m_arrived(d, half, d)

    for d in range(2):
        for s in range(1, hx + 1):
            for c in range(2) if s < hx else (d,):
                v_copy(d, s, c, 0).wait_send()
    for n, m in over:
        v_over(n, m, False).wait_send()
    c_drain()
    for d, c in chains:
        for s in range(1, length(d, c) + 1):
            r_copy(d, c, s).wait_send()
    pair.wait_send()
    for j in far:
        a_copy(j).wait_send()
        g_copy(j, False).wait_send()
    give.wait_send()
    m_drain()


def density_kernel(mix_ref, vt_ref, out_ref, lhs):
    count, tile = mix_ref.shape[0], mix_ref.shape[1]
    for n in range(count):
        lhs.at[n // 2][pl.ds(n % 2, tile, stride=2), :] = mix_ref[n].astype(F32)
    both = jnp.concatenate([lhs[n].astype(BF16) for n in range(count // 2)], axis=1)
    total = jnp.dot(both, vt_ref[...], preferred_element_type=F32)
    out_ref[...] = total.astype(BF16).reshape(out_ref.shape)


def per_device(nrow, ncol, perturbation, occ_coeffs, vir_coeffs, occ_energies, vir_energies):
    pert, rows, cols = perturbation.shape
    occ, vir = occ_energies.shape[0], vir_energies.shape[0]
    nocc, nx, half = occ_coeffs.shape[1], nrow // 2, ncol // 2
    padded = round_up(rows, 16)
    cut = round_up(padded // 2, 16)
    assert pert == 2 and pert * vir == ncol * LANES and nx == ncol and nocc <= 2 * LANES
    dma = pltpu.SemaphoreType.DMA
    ring = 2 * half - 1
    dims = (nrow, ncol, rows, cols, occ, vir)
    vmem = pl.BlockSpec(memory_space=pltpu.VMEM)
    mixed, vt_all = pl.pallas_call(
        functools.partial(exchange_kernel, dims),
        out_shape=(
            jax.ShapeDtypeStruct((ncol, padded, LANES), BF16),
            jax.ShapeDtypeStruct((vir, cols), BF16),
        ),
        in_specs=[pl.BlockSpec(memory_space=pl.ANY)] + [vmem] * 4,
        out_specs=(vmem, vmem),
        scratch_shapes=[
            pltpu.VMEM((rows, pert, cols), BF16),
            pltpu.VMEM((vir // LANES, 2 * padded, LANES), F32),
            pltpu.VMEM((ncol, padded, LANES), F32),
            pltpu.VMEM((ncol, padded, 2 * LANES), BF16),
            pltpu.VMEM((2, 2, cut, LANES), BF16),
            pltpu.VMEM((2, ring, cut, LANES), BF16),
            pltpu.VMEM((2, ncol, LANES, LANES), BF16),
            pltpu.VMEM((ncol, LANES, LANES), BF16),
            pltpu.VMEM((ncol, LANES, LANES), BF16),
            pltpu.VMEM((nx - 1, LANES, LANES), BF16),
            pltpu.VMEM((2, ncol, LANES, LANES), BF16),
            pltpu.VMEM((1, round_up(occ, LANES) + 2 * LANES), F32),
            dma,
            dma((2, ring)),
            dma((2, ring)),
            dma((nx,)),
            dma((nx,)),
            dma((2, ring)),
            dma((2, ring)),
            dma((2, ring)),
            dma((2, ring)),
            dma,
            dma,
            dma((nx - 1,)),
            dma((nx - 1,)),
            dma((nx - 1,)),
            dma((nx - 1,)),
            dma,
            dma,
            dma((2, ring)),
            dma((2, ring)),
        ],
        compiler_params=pltpu.CompilerParams(
            collective_id=0, has_side_effects=True, vmem_limit_bytes=56 * 2**20
        ),
        name="exchange",
    )(
        perturbation.transpose(1, 0, 2),
        vir_coeffs.T,
        occ_coeffs,
        occ_energies.reshape(1, occ),
        vir_energies.reshape(1, vir),
    )
    tile = 128
    density = pl.pallas_call(
        density_kernel,
        out_shape=jax.ShapeDtypeStruct((rows, pert, cols), BF16),
        grid=(-(-rows // tile),),
        in_specs=[
            pl.BlockSpec((ncol, tile, LANES), lambda i: (0, i, 0)),
            pl.BlockSpec((vir, cols), lambda i: (0, 0)),
        ],
        out_specs=pl.BlockSpec((tile, pert, cols), lambda i: (i, 0, 0)),
        scratch_shapes=[pltpu.VMEM((vir // LANES, pert * tile, LANES), F32)],
        compiler_params=pltpu.CompilerParams(vmem_limit_bytes=40 * 2**20),
        name="density",
    )(mixed, vt_all)
    return density.transpose(1, 0, 2)


def solution(mesh):
    spec = P("grp", "row", "col")
    return jax.shard_map(
        functools.partial(per_device, mesh.shape["row"], mesh.shape["col"]),
        mesh=mesh,
        in_specs=(spec, P("row", "col"), P("col", "row"), P(), P()),
        out_specs=spec,
        check_vma=False,
    )
```

time: 289 us -> 119 us (0.41)
  waiting for transfers between devices: 120 us -> 0 us
  Pallas kernels: 0 us -> 115 us
  blocking collectives: 72.1 us -> 0 us
  local copies, waits for them, and re-layouts: 38.9 us -> 2.8 us
  starting transfers between devices: 27.4 us -> 0 us
  between operations: 13.2 us -> 0.02 us
  matrix products: 12.2 us -> 0 us
  other arithmetic: 4.5 us -> 0 us
    pallas_call x0 -> x2, Pallas kernels: none -> 115 us  [the longest x1 109 us: per_device(): pl.pallas_call(functools.partial(exchange_kernel, dims), out_shape=(jax.S...]
    all_to_all x2 -> x0, waiting for transfers between devices: 64 us -> none  [the longest x1 35.1 us: sent_to_all(): return lax.all_to_all(copies, axis, split_axis=0, concat_axis=0, tiled=True)]
    reduce_scatter x2 -> x0, waiting for transfers between devices: 52.5 us -> none  [reduced_to_own(): pieces = lax.psum_scatter(pieces, axes[k], scatter_dimension=0, tiled=True)]
    all_to_all x1 -> x0, blocking collectives: 41.8 us -> none  [sent_to_all(): return lax.all_to_all(copies, axis, split_axis=0, concat_axis=0, tiled=True)]
    all_gather x2 -> x0, blocking collectives: 30.3 us -> none  [stacked_from(): pieces = lax.all_gather(pieces, axes[k], axis=0, tiled=True)]
    all_to_all x2 -> x0, starting transfers between devices: 27.3 us -> none  [the longest x1 22.8 us: sent_to_all(): return lax.all_to_all(copies, axis, split_axis=0, concat_axis=0, tiled=True)]
    dot_general x4 -> x0, matrix products: 12.2 us -> none  [the longest x1 4.95 us: per_device(): jnp.einsum('pij,jv->vpi', perturbation, vir_rows, preferred_element_type=...]
    another operation x3 -> x0, local copies, waits for them, and re-layouts: 9.93 us -> none  [the longest x2 6.28 us: reduced_to_own(): pieces = jnp.moveaxis(pieces, order, range(len(axes))).reshape(-1, *inside)]
  transfers between devices with their start and end apart: 5 -> 0, of which waited for: 5 -> 0; matrix products, arithmetic and copies ran while one was open for 6% -> 0% of each run, Pallas kernels for 0% -> 0%
where the time goes in v1:
time: 119 us; the launch traced here: 117 us
  Pallas kernels  115 us (97%)
  local copies, waits for them, and re-layouts  2.8 us (2%)
    pallas_call x1, Pallas kernels, per_device(): pl.pallas_call(functools.partial(exchange_kernel, dims), out_shape=(jax.S...  109 us
    pallas_call x1, Pallas kernels, per_device(): pl.pallas_call(density_kernel, out_shape=jax.ShapeDtypeStruct((rows, pert...  5.24 us
    unnamed x4, local copies, waits for them, and re-layouts  2.8 us

profile of v1, /device:TPU:516, one launch (start us, length us, event | category | flops | bytes accessed | tf_op | source)
XLA Modules:
  0.0 117.3 jit_solution(14640287746376982475)
XLA Ops:
  0.0 109.3 %exchange.1 = (bf16[8,752,128]{2,1,0:T(8,128)(2,1)}, bf16[512,1500]{1,0:T(8,128)(2,1)}) custom-call(bf16[750,2,1500]{2,1,0:T(2,128)(2,1)} %bitcast.5, bf16[32,1500]{1,0:T(8,128)(2,1)} %bitcast.6, bf16[750,250]{1,0:T(8,128)(2,1)} %refs_2_.1, f32[1,2000]{1,0:T(1,128)} %bitcast.7, f32[1,512]{1,0:T(1,128)} %bitcast.8), custom_call_target="tpu_custom_call" | custom-call | tf_op jit(solution)/shard_map/exchange/pallas_call | solution.py:317
  109.3 0.0 copy-start
  109.3 1.4 %copy-done = bf16[512,1500]{1,0:T(8,128)(2,1)S(1)} copy-done((bf16[512,1500]{1,0:T(8,128)(2,1)S(1)}, bf16[512,1500]{1,0:T(8,128)(2,1)}, u32[]{:S(2)}) %copy-start) | copy-done | bytes 1536024
  110.7 0.0 copy-start.1
  110.7 1.4 %copy-done.1 = bf16[8,752,128]{2,1,0:T(8,128)(2,1)S(1)} copy-done((bf16[8,752,128]{2,1,0:T(8,128)(2,1)S(1)}, bf16[8,752,128]{2,1,0:T(8,128)(2,1)}, u32[]{:S(2)}) %copy-start.1) | copy-done | bytes 1540120
  112.1 5.2 %density.1 = bf16[750,2,1500]{2,1,0:T(2,128)(2,1)} custom-call(bf16[8,752,128]{2,1,0:T(8,128)(2,1)S(1)} %copy-done.1, bf16[512,1500]{1,0:T(8,128)(2,1)S(1)} %copy-done), custom_call_target="tpu_custom_call" | custom-call | tf_op jit(solution)/shard_map/density/pallas_call | solution.py:370
Async XLA Ops:
  109.3 1.4 %copy-start = (bf16[512,1500]{1,0:T(8,128)(2,1)S(1)}, bf16[512,1500]{1,0:T(8,128)(2,1)}, u32[]{:S(2)}) copy-start(bf16[512,1500]{1,0:T(8,128)(2,1)} %get-tuple-element.8.vt_ref) | copy-start | bytes 4608004
  110.7 1.4 %copy-start.1 = (bf16[8,752,128]{2,1,0:T(8,128)(2,1)S(1)}, bf16[8,752,128]{2,1,0:T(8,128)(2,1)}, u32[]{:S(2)}) copy-start(bf16[8,752,128]{2,1,0:T(8,128)(2,1)} %get-tuple-element.7.mix_ref) | copy-start | bytes 4620292
